TPU v7x, 32 devices: a whole 2x2x4 slice. The times are simulated.
32 devices in a mesh: fsdp: 8 (over z, x), grp: 4 (over y, core).
Axes of the slice: x: 2, y: 2, z: 4, core: 2. Of those that a mesh axis runs over, the one named last changes fastest.
Arguments:
- gradient: bfloat16 [24, 512, 512], P('fsdp', 'grp'), may hold values from -6 to 6
- left_factor: bfloat16 [96, 512, 512], P(('fsdp', 'grp'))
- right_factor: bfloat16 [96, 512, 512], P(('fsdp', 'grp'))
- block_owner: int32 [24], replicated, may hold values from 0 to 31, as said below
Outputs:
- preconditioned: bfloat16 [24, 512, 512], P('fsdp', 'grp')
Inputs may be any that keep to these rules, and one draw needn't show every extreme that they name: block_owner[b] is a device index, fsdp index times 4 plus grp index. The 3 blocks homed at one fsdp index go to devices of 3 different fsdp indices; the devices of each fsdp index own 3 blocks in all; no device owns more than 3 blocks, and at every fsdp index one device owns exactly 3.
All inputs are finite; a program needn't handle non-finite values.
Results may differ from a plain program's by a relative error of at most 0.0049.
Values may be sent and summed in bfloat16 or wider, within the bound.
A program may use at most 64 MiB of HBM per device.

v0:
```python
import jax
import jax.numpy as jnp
from jax import lax
from jax.sharding import PartitionSpec as P


def per_device(gradient, left_factor, right_factor, block_owner):
    local_blocks = gradient.shape[0]
    piece_rows = gradient.shape[1]
    block_width = gradient.shape[2]
    slot_count = left_factor.shape[0]
    columns = lax.axis_size("fsdp")
    groups = lax.axis_size("grp")
    column = lax.axis_index("fsdp")
    owners_all = block_owner.reshape(columns, local_blocks)
    dest_column = owners_all // groups
    dest_group = owners_all % groups
    mine_column = lax.dynamic_index_in_dim(dest_column, column, 0, keepdims=False)
    column_ids = jnp.arange(columns, dtype=jnp.int32)
    matching = mine_column[None, :] == column_ids[:, None]
    pick_send = matching.astype(jnp.bfloat16)
    outgoing = jnp.einsum(
        "cj,jrd->crd", pick_send, gradient, preferred_element_type=jnp.float32
    ).astype(jnp.bfloat16)
    arrived = lax.all_to_all(
        outgoing.reshape(columns * piece_rows, block_width),
        "fsdp",
        split_axis=0,
        concat_axis=0,
        tiled=True,
    )
    arrived = arrived.reshape(columns, piece_rows, block_width)
    toward = dest_column == column
    live_source = jnp.sum(toward.astype(jnp.int32), axis=1) > 0
    target = jnp.sum(jnp.where(toward, dest_group, 0), axis=1)
    same_owner = (target[None, :] == target[:, None]) & live_source[None, :] & live_source[:, None]
    before = column_ids[None, :] < column_ids[:, None]
    rank_slot = jnp.sum((same_owner & before).astype(jnp.int32), axis=1)
    group_ids = jnp.arange(groups, dtype=jnp.int32)
    slot_ids = jnp.arange(slot_count, dtype=jnp.int32)
    routing = (
        live_source[None, None, :]
        & (target[None, None, :] == group_ids[:, None, None])
        & (rank_slot[None, None, :] == slot_ids[None, :, None])
    )
    routing = routing.astype(jnp.bfloat16)
    packed = jnp.einsum(
        "oks,srd->kord", routing, arrived, preferred_element_type=jnp.float32
    ).astype(jnp.bfloat16)
    packed = packed.reshape(slot_count, groups * piece_rows, block_width)
    blocks = lax.all_to_all(packed, "grp", split_axis=1, concat_axis=1, tiled=True)
    left_product = jnp.einsum(
        "kab,kbc->kac", left_factor, blocks, preferred_element_type=jnp.float32
    ).astype(jnp.bfloat16)
    result = jnp.einsum(
        "kab,kbc->kac", left_product, right_factor, preferred_element_type=jnp.float32
    ).astype(jnp.bfloat16)
    returned = lax.all_to_all(result, "grp", split_axis=1, concat_axis=1, tiled=True)
    returned = returned.reshape(slot_count, groups, piece_rows, block_width)
    unpacked = jnp.einsum(
        "oks,kord->srd", routing, returned, preferred_element_type=jnp.float32
    ).astype(jnp.bfloat16)
    homeward = lax.all_to_all(
        unpacked.reshape(columns * piece_rows, block_width),
        "fsdp",
        split_axis=0,
        concat_axis=0,
        tiled=True,
    )
    homeward = homeward.reshape(columns, piece_rows, block_width)
    return jnp.einsum(
        "cj,crd->jrd", pick_send, homeward, preferred_element_type=jnp.float32
    ).astype(jnp.bfloat16)


def solution(mesh):
    return jax.shard_map(
        per_device,
        mesh=mesh,
        in_specs=(
            P("fsdp", "grp", None),
            P(("fsdp", "grp"), None, None),
            P(("fsdp", "grp"), None, None),
            P(),
        ),
        out_specs=P("fsdp", "grp", None),
        check_vma=False,
    )
```

profile of v0, /device:TPU:0, one launch (start us, length us, event | category | flops | bytes accessed | tf_op | source)
XLA Modules:
  0.0 135.2 jit_solution(5954696607277778726)
XLA Ops:
  0.0 0.0 copy-start
  0.0 0.8 reshape.94
  0.9 1.6 %convolution_convert_fusion.3 = bf16[8,128,512]{2,0,1:T(8,128)(2,1)S(1)} fusion(bf16[3,128,512]{2,1,0:T(8,128)(2,1)} %param.4, s32[3]{0:T(128)S(1)} %dynamic-slice_bitcast_fusion), kind=kOutput, calls=%fused_computation.7 | convolution fusion | flops 3670040 | bytes 1441804 | tf_op jit(solution)/shard_map/cj,jrd->crd/dot_general | solution.py:22
  2.5 1.3 copy.33
  3.8 7.3 %all-to-all-start = ((bf16[8,128,512]{2,1,0:T(8,128)(2,1)}), bf16[8,128,512]{2,1,0:T(8,128)(2,1)S(1)}, u32[]{:S(2)}, u32[]{:S(2)}) async-start(bf16[8,128,512]{2,1,0:T(8,128)(2,1)} %copy.33), calls=%async_computation | async-start | bytes 2097152 | tf_op jit(solution)/shard_map/all_to_all | solution.py:25
  11.1 0.1 convert_reduce_fusion.1
  11.2 0.2 convert_reduce_fusion
  11.4 25.4 %all-to-all-done = bf16[8,128,512]{2,1,0:T(8,128)(2,1)S(1)} async-done(((bf16[8,128,512]{2,1,0:T(8,128)(2,1)}), bf16[8,128,512]{2,1,0:T(8,128)(2,1)S(1)}, u32[]{:S(2)}, u32[]{:S(2)}) %all-to-all-start) | async-done | bytes 1048608 | tf_op jit(solution)/shard_map/all_to_all | solution.py:25
  36.8 1.0 fusion.2
  37.9 0.3 copy.35
  38.2 1.4 copy.36
  39.6 28.9 %all_to_all.22 = bf16[3,512,512]{2,0,1:T(4,128)(2,1)} all-to-all(bf16[3,512,512]{2,0,1:T(4,128)(2,1)S(1)} %copy.36), channel_id=1, replica_groups=mesh['fsdp'=8,'grp'=4] {'grp'}, dimensions={1} | all-to-all | bytes 3145728 | tf_op jit(solution)/shard_map/all_to_all | solution.py:51
  68.5 0.0 copy-done
  68.5 4.2 %convolution_convert_fusion = bf16[3,512,512]{2,1,0:T(8,128)(2,1)S(1)} fusion(bf16[3,512,512]{2,1,0:T(8,128)(2,1)S(1)} %copy-done, bf16[3,512,512]{2,1,0:T(8,128)(2,1)} %param.5, bf16[3,512,512]{2,0,1:T(4,128)(2,1)} %all_to_all.22), kind=kOutput, calls=%fused_computation.1 | convolution fusion | flops 1612185600 | bytes 6291456 | tf_op jit(solution)/shard_map/kab,kbc->kac/dot_general | solution.py:55
  72.7 1.4 copy.39
  74.0 28.1 %all_to_all.23 = bf16[3,512,512]{2,0,1:T(4,128)(2,1)S(1)} all-to-all(bf16[3,512,512]{2,0,1:T(4,128)(2,1)S(1)} %copy.39), channel_id=1, replica_groups=mesh['fsdp'=8,'grp'=4] {'grp'}, dimensions={1} | all-to-all | bytes 3145728 | tf_op jit(solution)/shard_map/all_to_all | solution.py:58
  102.2 2.2 %bitcast_convert_fusion = bf16[8,128,512]{2,0,1:T(8,128)(2,1)S(1)} fusion(bf16[3,4,128,512]{3,0,2,1:T(4,128)(2,1)S(1)} %bitcast.23, pred[3,8]{1,0:T(4,128)(4,1)S(1)} %iota_compare_fusion.1, pred[4,8]{1,0:T(4,128)(4,1)S(1)} %fusion.22), kind=kOutput, calls=%fused_computation | convolution fusion | flops 13107296 | bytes 2621496 | tf_op jit(solution)/shard_map/oks,kord->srd/dot_general | solution.py:60
  104.4 0.3 copy.42
  104.7 28.8 %all_to_all.24 = bf16[8,128,512]{2,1,0:T(8,128)(2,1)S(1)} all-to-all(bf16[8,128,512]{2,1,0:T(8,128)(2,1)S(1)} %copy.42), channel_id=1, replica_groups=mesh['fsdp'=8,'grp'=4] {'fsdp'}, dimensions={0} | all-to-all | bytes 2097152 | tf_op jit(solution)/shard_map/all_to_all | solution.py:63
  133.6 0.8 convolution_convert_fusion.4
  134.4 0.8 copy.44
  (5 shorter events, 0.0 us)
Async XLA Ops:
  0.0 68.5 %copy-start = (bf16[3,512,512]{2,1,0:T(8,128)(2,1)S(1)}, bf16[3,512,512]{2,1,0:T(8,128)(2,1)}, u32[]{:S(2)}) copy-start(bf16[3,512,512]{2,1,0:T(8,128)(2,1)} %param.6) | copy-start | bytes 4718596
  3.8 33.0 %all-to-all-start = ((bf16[8,128,512]{2,1,0:T(8,128)(2,1)}), bf16[8,128,512]{2,1,0:T(8,128)(2,1)S(1)}, u32[]{:S(2)}, u32[]{:S(2)}) async-start(bf16[8,128,512]{2,1,0:T(8,128)(2,1)} %copy.33), calls=%async_computation | async-start | bytes 2097152 | tf_op jit(solution)/shard_map/all_to_all | solution.py:25
where the time goes:
time: 136 us; the launch traced here: 135 us
  blocking collectives  85.9 us (63%)
  waiting for transfers between devices  25.4 us (19%)
  matrix products  9.85 us (7%)
  starting transfers between devices  7.28 us (5%)
  local copies, waits for them, and re-layouts  6.34 us (5%)
    all_to_all x1, blocking collectives, per_device(): lax.all_to_all(packed, 'grp', split_axis=1, concat_axis=1, tiled=True)  28.9 us
    all_to_all x1, blocking collectives, per_device(): lax.all_to_all(unpacked.reshape(columns * piece_rows, block_width), 'fsdp...  28.8 us
    all_to_all x1, blocking collectives, per_device(): lax.all_to_all(result, 'grp', split_axis=1, concat_axis=1, tiled=True)  28.1 us
    all_to_all x1, waiting for transfers between devices, per_device(): lax.all_to_all(outgoing.reshape(columns * piece_rows, block_width), 'fsdp...  25.4 us
    all_to_all x1, starting transfers between devices, per_device(): lax.all_to_all(outgoing.reshape(columns * piece_rows, block_width), 'fsdp...  7.28 us
    dot_general x1, matrix products, per_device(): jnp.einsum('kab,kbc->kac', left_product, right_factor, preferred_element_...  4.21 us
  transfers between devices with their start and end apart: 1, of which 1 were waited for; matrix products, arithmetic and copies ran while one was open for 0% of the time, Pallas kernels for 0%

commit v1 on v0

--- a/solution.py
+++ b/solution.py
@@ -55,7 +55,10 @@
     result = jnp.einsum(
         "kab,kbc->kac", left_product, right_factor, preferred_element_type=jnp.float32
     ).astype(jnp.bfloat16)
-    returned = lax.all_to_all(result, "grp", split_axis=1, concat_axis=1, tiled=True)
+    returned = jnp.concatenate(
+        lax.all_to_all(jnp.stack(jnp.split(result, lax.axis_size("grp"), axis=1)), "grp", 0, 0),
+        axis=1,
+    )
     returned = returned.reshape(slot_count, groups, piece_rows, block_width)
     unpacked = jnp.einsum(
         "oks,kord->srd", routing, returned, preferred_element_type=jnp.float32

time: 136 us -> 129 us (0.949)
  blocking collectives: 85.9 us -> 80.2 us
    all_to_all x1, blocking collectives: 28.1 us -> 22.5 us  [per_device(): lax.all_to_all(jnp.stack(jnp.split(result, lax.axis_size('grp'), axis=1))...]
where the time goes in v1:
time: 129 us; the launch traced here: 128 us
  blocking collectives  80.2 us (62%)
  waiting for transfers between devices  25.4 us (20%)
  matrix products  9.55 us (7%)
  starting transfers between devices  7.28 us (6%)
  local copies, waits for them, and re-layouts  5.16 us (4%)
    all_to_all x1, blocking collectives, per_device(): lax.all_to_all(packed, 'grp', split_axis=1, concat_axis=1, tiled=True)  28.9 us
    all_to_all x1, blocking collectives, per_device(): lax.all_to_all(unpacked.reshape(columns * piece_rows, block_width), 'fsdp...  28.8 us
    all_to_all x1, waiting for transfers between devices, per_device(): lax.all_to_all(outgoing.reshape(columns * piece_rows, block_width), 'fsdp...  25.4 us
    all_to_all x1, blocking collectives, per_device(): lax.all_to_all(jnp.stack(jnp.split(result, lax.axis_size('grp'), axis=1))...  22.5 us
    all_to_all x1, starting transfers between devices, per_device(): lax.all_to_all(outgoing.reshape(columns * piece_rows, block_width), 'fsdp...  7.28 us
    dot_general x1, matrix products, per_device(): jnp.einsum('kab,kbc->kac', left_product, right_factor, preferred_element_...  4.21 us
  transfers between devices with their start and end apart: 1, of which 1 were waited for; matrix products, arithmetic and copies ran while one was open for 0% of the time, Pallas kernels for 0%

profile of v1, /device:TPU:0, one launch (start us, length us, event | category | flops | bytes accessed | tf_op | source)
XLA Modules:
  0.0 128.3 jit_solution(15645042587539966793)
XLA Ops:
  0.0 0.0 copy-start
  0.0 0.8 reshape.94
  0.9 1.6 %convolution_convert_fusion.3 = bf16[8,128,512]{2,0,1:T(8,128)(2,1)S(1)} fusion(bf16[3,128,512]{2,1,0:T(8,128)(2,1)} %param.4, s32[3]{0:T(128)S(1)} %dynamic-slice_bitcast_fusion), kind=kOutput, calls=%fused_computation.8 | convolution fusion | flops 3670040 | bytes 1441804 | tf_op jit(solution)/shard_map/cj,jrd->crd/dot_general | solution.py:22
  2.5 1.3 %copy.20 = bf16[8,128,512]{2,1,0:T(8,128)(2,1)} copy(bf16[8,128,512]{2,0,1:T(8,128)(2,1)S(1)} %convolution_convert_fusion.3) | data formatting | bytes 2097152 | tf_op jit(solution)/shard_map/convert_element_type | solution.py:24
  3.8 7.3 %all-to-all-start = ((bf16[8,128,512]{2,1,0:T(8,128)(2,1)}), bf16[8,128,512]{2,1,0:T(8,128)(2,1)S(1)}, u32[]{:S(2)}, u32[]{:S(2)}) async-start(bf16[8,128,512]{2,1,0:T(8,128)(2,1)} %copy.20), calls=%async_computation | async-start | bytes 2097152 | tf_op jit(solution)/shard_map/all_to_all | solution.py:25
  11.1 0.1 convert_reduce_fusion.1
  11.2 0.2 convert_reduce_fusion
  11.4 25.4 %all-to-all-done = bf16[8,128,512]{2,1,0:T(8,128)(2,1)S(1)} async-done(((bf16[8,128,512]{2,1,0:T(8,128)(2,1)}), bf16[8,128,512]{2,1,0:T(8,128)(2,1)S(1)}, u32[]{:S(2)}, u32[]{:S(2)}) %all-to-all-start) | async-done | bytes 1048608 | tf_op jit(solution)/shard_map/all_to_all | solution.py:25
  36.8 1.0 fusion.2
  37.9 0.3 copy.22
  38.2 1.4 %copy.23 = bf16[3,512,512]{2,0,1:T(4,128)(2,1)S(1)} copy(bf16[3,512,512]{2,1,0:T(8,128)(2,1)S(1)} %bitcast.29) | data formatting | bytes 3145728 | tf_op jit(solution)/shard_map/reshape | solution.py:50
  39.6 28.9 %all_to_all.22 = bf16[3,512,512]{2,0,1:T(4,128)(2,1)} all-to-all(bf16[3,512,512]{2,0,1:T(4,128)(2,1)S(1)} %copy.23), channel_id=1, replica_groups=mesh['fsdp'=8,'grp'=4] {'grp'}, dimensions={1} | all-to-all | bytes 3145728 | tf_op jit(solution)/shard_map/all_to_all | solution.py:51
  68.5 0.0 copy-done
  68.5 4.2 %convolution_convert_fusion = bf16[3,512,512]{2,1,0:T(8,128)(2,1)S(1)} fusion(bf16[3,512,512]{2,1,0:T(8,128)(2,1)S(1)} %copy-done, bf16[3,512,512]{2,1,0:T(8,128)(2,1)} %param.5, bf16[3,512,512]{2,0,1:T(4,128)(2,1)} %all_to_all.22), kind=kOutput, calls=%fused_computation.1 | convolution fusion | flops 1612185600 | bytes 6291456 | tf_op jit(solution)/shard_map/kab,kbc->kac/dot_general | solution.py:55
  72.7 0.2 slice_bitcast_fusion.3
  72.9 0.2 pad_maximum_fusion
  73.1 22.5 %all_to_all.23 = bf16[4,3,128,512]{3,2,1,0:T(8,128)(2,1)S(1)} all-to-all(bf16[4,3,128,512]{3,2,1,0:T(8,128)(2,1)S(1)} %pad_maximum_fusion), channel_id=1, replica_groups=mesh['fsdp'=8,'grp'=4] {'grp'}, dimensions={0} | all-to-all | bytes 3145728 | tf_op jit(solution)/shard_map/all_to_all | solution.py:59
  95.6 1.9 %bitcast_convert_fusion = bf16[8,128,512]{2,0,1:T(8,128)(2,1)S(1)} fusion(bf16[3,4,128,512]{3,2,0,1:T(8,128)(2,1)S(1)} %bitcast.31, pred[3,8]{1,0:T(4,128)(4,1)S(1)} %iota_compare_fusion.1, pred[4,8]{1,0:T(4,128)(4,1)S(1)} %fusion.22), kind=kOutput, calls=%fused_computation | convolution fusion | flops 13107296 | bytes 2621496 | tf_op jit(solution)/shard_map/oks,kord->srd/dot_general | solution.py:63
  97.5 0.3 copy.27
  97.8 28.8 %all_to_all.24 = bf16[8,128,512]{2,1,0:T(8,128)(2,1)S(1)} all-to-all(bf16[8,128,512]{2,1,0:T(8,128)(2,1)S(1)} %copy.27), channel_id=1, replica_groups=mesh['fsdp'=8,'grp'=4] {'fsdp'}, dimensions={0} | all-to-all | bytes 2097152 | tf_op jit(solution)/shard_map/all_to_all | solution.py:66
  126.7 0.8 convolution_convert_fusion.4
  127.5 0.8 copy.29
  (5 shorter events, 0.0 us)
Async XLA Ops:
  0.0 68.5 %copy-start = (bf16[3,512,512]{2,1,0:T(8,128)(2,1)S(1)}, bf16[3,512,512]{2,1,0:T(8,128)(2,1)}, u32[]{:S(2)}) copy-start(bf16[3,512,512]{2,1,0:T(8,128)(2,1)} %param.6) | copy-start | bytes 4718596
  3.8 33.0 %all-to-all-start = ((bf16[8,128,512]{2,1,0:T(8,128)(2,1)}), bf16[8,128,512]{2,1,0:T(8,128)(2,1)S(1)}, u32[]{:S(2)}, u32[]{:S(2)}) async-start(bf16[8,128,512]{2,1,0:T(8,128)(2,1)} %copy.20), calls=%async_computation | async-start | bytes 2097152 | tf_op jit(solution)/shard_map/all_to_all | solution.py:25
